TPU v7x, 32 devices: a whole 2x2x4 slice. The times are simulated.
32 devices in a mesh: dp: 4 (over z), mp: 8 (over y, x, core).
Axes of the slice: x: 2, y: 2, z: 4, core: 2. Of those that a mesh axis runs over, the one named last changes fastest.
Arguments:
- tokens: bfloat16 [4096, 4096], P('dp', 'mp'), may hold values from -6 to 6
- decay: float32 [4096, 16], P('dp'), may hold values from 0.75 to 1, as said below
- state: float32 [128, 256, 8192], P('dp', None, 'mp'), may hold values from -24 to 24
- w_query: bfloat16 [4096, 4096], P(None, 'mp'), may hold values from -0.09375 to 0.09375
- w_key: bfloat16 [4096, 4096], P(None, 'mp'), may hold values from -0.09375 to 0.09375
- w_value: bfloat16 [4096, 8192], P(None, 'mp'), may hold values from -0.09375 to 0.09375
- w_gate: bfloat16 [4096, 8192], P(None, 'mp'), may hold values from -0.09375 to 0.09375
- w_out: bfloat16 [8192, 4096], P('mp'), may hold values from -0.09375 to 0.09375
- norm_gain: float32 [8192], P('mp'), may hold values from 0.25 to 1.75
Outputs:
- layer_out: bfloat16 [4096, 4096], P('dp', 'mp')
- new_state: float32 [128, 256, 8192], P('dp', None, 'mp')
Inputs may be any that keep to these rules, and one draw needn't show every extreme that they name: `decay`: each head has its own base rate over all tokens, varied somewhat from token to token.
All inputs are finite; a program needn't handle non-finite values.
Results may differ from a plain program's by a relative error of at most 0.0071.
Values may be sent and summed in bfloat16 or wider, within the bound.
A program may use at most 256 MiB of HBM per device.

v0:
```python
import jax
import jax.numpy as jnp
from jax import lax
from jax.sharding import PartitionSpec as P

HEAD = 256
VHEAD = 512
NEW = 32


EPS = 0.1


def partner(shard, axis, bit):
    return lax.ppermute(shard, axis, [(i, i ^ 1 << bit) for i in range(lax.axis_size(axis))])


def per_device(tokens, decay, state, w_query, w_key, w_value, w_gate, w_out, norm_gain):
    highest = lax.Precision.HIGHEST
    tok_rows = tokens.shape[0]
    qk_columns = w_query.shape[1]
    v_columns = w_value.shape[1]
    head_span = max(1, HEAD // qk_columns)
    groups = max(1, qk_columns // HEAD)
    qk_width = qk_columns // groups
    v_width = v_columns // groups
    sequences = tok_rows // NEW
    bit_count = head_span.bit_length() - 1
    device_index = lax.axis_index("mp")
    first_head = device_index * qk_columns // HEAD
    qk_zeros = jnp.zeros((tok_rows, qk_columns), jnp.float32)
    v_zeros = jnp.zeros((tok_rows, v_columns), jnp.float32)
    carried = (qk_zeros, qk_zeros, v_zeros, v_zeros)
    segment = lax.all_gather(tokens, "mp", axis=1, tiled=True)
    updated = []
    for running, weight in zip(carried, (w_query, w_key, w_value, w_gate)):
        updated.append(jnp.dot(segment, weight, preferred_element_type=jnp.float32))
    query, key_proj, value_proj, gate_proj = tuple(updated)
    query = (query * HEAD ** (-0.5)).astype(jnp.bfloat16).reshape(tok_rows, groups, qk_width)
    key_proj = key_proj.astype(jnp.bfloat16).reshape(tok_rows, groups, qk_width)
    value_proj = value_proj.astype(jnp.bfloat16)
    for bit_number in range(bit_count):
        other_query, other_key = partner((query, key_proj), "mp", bit_number)
        upper_half = device_index >> bit_number & 1 == 1
        query = jnp.where(
            upper_half,
            jnp.concatenate([other_query, query], 2),
            jnp.concatenate([query, other_query], 2),
        )
        key_proj = jnp.where(
            upper_half,
            jnp.concatenate([other_key, key_proj], 2),
            jnp.concatenate([key_proj, other_key], 2),
        )
    query_block = query.reshape(sequences, NEW, groups, HEAD)
    key_block = key_proj.reshape(sequences, NEW, groups, HEAD)
    value_block = value_proj.reshape(sequences, NEW, groups, v_width)
    decay_rates = lax.dynamic_slice_in_dim(decay, first_head, groups, 1).reshape(
        sequences, NEW, groups
    )
    log_cumul = jnp.cumsum(jnp.log(decay_rates), axis=1)
    old_state = state.reshape(sequences, HEAD, groups, v_width)
    from_state = jnp.einsum(
        "bngk,bkgv->bngv", query_block.astype(jnp.float32), old_state, precision=highest
    )
    scores = jnp.einsum(
        "bngk,bmgk->bgnm", query_block, key_block, preferred_element_type=jnp.float32
    )
    along = jnp.transpose(log_cumul, (0, 2, 1))
    log_gap = along[:, :, :, None] - along[:, :, None, :]
    causal = jnp.arange(NEW)[:, None] >= jnp.arange(NEW)[None, :]
    factor = jnp.where(causal, jnp.exp(jnp.where(causal, log_gap, 0.0)), 0.0)
    weights = (scores * factor).astype(jnp.bfloat16)
    in_block = jnp.einsum(
        "bgnm,bmgv->bngv", weights, value_block, preferred_element_type=jnp.float32
    )
    retained = jnp.exp(log_cumul)[..., None] * from_state + in_block
    final_log = log_cumul[:, -1, :]
    carry_scale = jnp.exp(final_log[:, None, :] - log_cumul)
    decayed_keys = key_block.astype(jnp.float32) * carry_scale[..., None]
    fresh = jnp.einsum(
        "bngk,bngv->bkgv", decayed_keys, value_block.astype(jnp.float32), precision=highest
    )
    new_state = jnp.exp(final_log)[:, None, :, None] * old_state + fresh
    new_state = new_state.reshape(sequences, HEAD, v_columns)
    retained = retained.reshape(tok_rows, groups, v_width)
    running = jnp.sum(retained, axis=-1)
    squares = jnp.sum(retained * retained, axis=-1)
    for bit_number in range(bit_count):
        other_sum, other_square = partner((running, squares), "mp", bit_number)
        running = running + other_sum
        squares = squares + other_square
    centre = running / VHEAD
    variance = squares / VHEAD - centre * centre
    deviation = retained - centre[..., None]
    normed = deviation * lax.rsqrt(variance + EPS)[..., None]
    gated_out = (normed.reshape(tok_rows, v_columns) * norm_gain * jax.nn.silu(gate_proj)).astype(
        jnp.bfloat16
    )
    partial_terms = jnp.dot(gated_out, w_out, preferred_element_type=jnp.float32)
    layer_out = lax.psum_scatter(partial_terms, "mp", scatter_dimension=1, tiled=True).astype(
        jnp.bfloat16
    )
    return (layer_out, new_state)


def solution(mesh):
    placed = (
        P("dp", "mp"),
        P("dp", None),
        P("dp", None, "mp"),
        P(None, "mp"),
        P(None, "mp"),
        P(None, "mp"),
        P(None, "mp"),
        P("mp", None),
        P("mp"),
    )
    return jax.shard_map(
        per_device,
        mesh=mesh,
        in_specs=placed,
        out_specs=(P("dp", "mp"), P("dp", None, "mp")),
        check_vma=False,
    )
```

profile of v0, /device:TPU:0, one launch (start us, length us, event | category | flops | bytes accessed | tf_op | source)
XLA Modules:
  0.0 312.2 jit_solution(14913403613981106068)
XLA Ops:
  7.2 0.0 all-gather.2.cloned.1.call-start
  7.2 0.7 all-gather.2.cloned.1.call-update
  7.9 0.0 reduce-scatter.2.cloned.1.call-start
  8.0 0.9 dynamic-slice_log_fusion
  8.8 0.1 log.7
  8.9 0.5 copy.82
  9.5 2.0 fusion.33
  11.5 0.4 copy.89
  11.8 33.6 %copy.84 = f32[32,256,1024]{1,2,0:T(8,128)} copy(f32[32,256,1024]{2,1,0:T(8,128)} %param.11) | data formatting | bytes 67108864 | tf_op args[2]
  45.5 0.1 copy.97
  45.6 0.0 copy-start.2
  45.6 0.6 copy-done.2
  46.1 0.1 copy.100
  46.2 0.9 subtract_exponential_fusion
  47.2 0.4 copy.83
  47.5 20.9 %all-gather.2.cloned.1.call-done = bf16[1024,4096]{1,0:T(8,128)(2,1)} async-done(((bf16[1024,512]{1,0:T(8,128)(2,1)}), bf16[1024,4096]{1,0:T(8,128)(2,1)}) %all-gather.2.cloned.1.call-update) | async-done | bytes 8388624 | tf_op jit(solution)/shard_map/all_gather | solution.py:34
  68.5 14.7 %convolution_convert_fusion = bf16[1024,1024]{1,0:T(8,128)(2,1)} fusion(bf16[1024,4096]{1,0:T(8,128)(2,1)} %all-gather.2.cloned.1.call-done, bf16[4096,1024]{1,0:T(8,128)(2,1)} %param.14), kind=kOutput, calls=%fused_computation.11 | convolution fusion | flops 8590983168 | bytes 18874368 | tf_op jit(solution)/shard_map/dot_general | solution.py:37
  83.1 3.3 %reshape.64 = bf16[32,32,2,512]{3,2,1,0:T(2,128)(2,1)S(1)} reshape(bf16[1024,1024]{1,0:T(8,128)(2,1)} %convolution_convert_fusion) | data formatting | bytes 4194304 | tf_op jit(solution)/shard_map/reshape | solution.py:57
  86.5 10.0 %convolution_convert_fusion.1 = bf16[1024,512]{1,0:T(8,128)(2,1)} fusion(bf16[1024,4096]{1,0:T(8,128)(2,1)} %all-gather.2.cloned.1.call-done, bf16[4096,512]{1,0:T(8,128)(2,1)} %param.13), kind=kOutput, calls=%fused_computation.14 | convolution fusion | flops 4295491584 | bytes 13631488 | tf_op jit(solution)/shard_map/dot_general | solution.py:37
  96.5 1.3 reshape_reshape.7
  97.8 10.0 %multiply_convert_fusion.2 = bf16[1024,512]{1,0:T(8,128)(2,1)} fusion(bf16[1024,4096]{1,0:T(8,128)(2,1)} %all-gather.2.cloned.1.call-done, bf16[4096,512]{1,0:T(8,128)(2,1)} %param.12), kind=kOutput, calls=%fused_computation.10 | convolution fusion | flops 4296015872 | bytes 13631488 | tf_op jit(solution)/shard_map/dot_general | solution.py:37
  107.9 2.2 reshape_reshape.6
  110.1 21.4 %fusion.18 = f32[32,2,32,512]{3,2,1,0:T(8,128)} fusion(f32[32,256,2,512]{1,3,2,0:T(8,128)} %bitcast.37, bf16[32,32,2,256]{3,2,1,0:T(2,128)(2,1)} %reshape_reshape.6), kind=kOutput, calls=%fused_computation.25 | convolution fusion | flops 3221225472 | bytes 38797312 | tf_op jit(solution)/shard_map/bngk,bkgv->bngv/dot_general | solution.py:63
  131.5 4.9 %fusion.26 = (f32[32,32,2]{1,2,0:T(2,128)S(1)}, f32[32,32,2]{1,2,0:T(2,128)S(1)}, f32[32,32,2,512]{3,1,2,0:T(8,128)}) fusion(bf16[32,32,2,512]{3,2,1,0:T(2,128)(2,1)S(1)} %reshape.64, bf16[32,32,2,256]{3,2,1,0:T(2,128)(2,1)S(1)} %reshape_reshape.7, bf16[32,32,2,256]{3,2,1,0:T(2,128)(2,1)} %reshape_reshape.6, f32[32,2,32]{2,1,0:T(2,128)S(1)} %copy.89, ...), kind=kOutput, calls=%fused_computation.40 | convolution fusion | flops 106229760 | bytes 12616704 | tf_op jit(solution)/shard_map/bgnm,bmgv->bngv/dot_general | solution.py:74
  136.4 0.1 div.28
  136.5 0.1 div.26
  136.6 1.0 copy.94
  137.7 1.0 copy.96
  138.7 2.9 mul.81
  141.6 0.0 copy-start
  141.6 3.0 copy.107
  144.6 0.0 copy-done
  144.6 3.3 %copy.92 = f32[32,32,2,512]{3,2,1,0:T(2,128)S(1)} copy(f32[32,32,2,512]{3,1,2,0:T(8,128)S(1)} %copy-done) | data formatting | bytes 8388608 | tf_op jit(solution)/shard_map/add | solution.py:77
  147.9 0.0 copy-start.1
  147.9 3.0 copy.105
  150.9 0.0 copy-done.1
  150.9 1.4 sub.51
  152.3 0.0 copy-start.4
  152.3 2.9 copy.106
  155.2 0.0 copy-done.4
  155.2 31.2 %fusion = f32[1024,4096]{1,0:T(8,128)} fusion(bf16[1024,4096]{1,0:T(8,128)(2,1)} %param.16, f32[1024,1024]{1,0:T(8,128)} %bitcast.44, f32[1024,1024]{1,0:T(8,128)} %bitcast.45, f32[1024,1024]{1,0:T(8,128)} %bitcast.46, f32[1024]{0:T(1024)S(1)} %copy-done.4, bf16[1024,4096]{1,0:T(8,128)(2,1)} %all-gather.2.cloned.1.call-done, bf16[4096,1024]{1,0:T(8,128)(2,1)} %param.15), kind=kOutput, calls=%fused_computation.5 | convolution fusion | flops 17189306368 | bytes 54530048 | tf_op jit(solution)/shard_map/dot_general | solution.py:100
  186.5 0.0 copy-start.3
  186.5 0.0 reduce-scatter.2.cloned.1.call-update
  186.5 0.6 copy-done.3
  187.2 0.1 copy.98
  187.2 1.4 copy.101
  188.6 28.9 %bitcast_add_fusion = f32[32,256,2,512]{1,3,2,0:T(8,128)} fusion(f32[32,256,2,512]{1,3,2,0:T(8,128)} %bitcast.38, f32[32,2]{1,0:T(8,128)S(1)} %copy.98, bf16[32,32,2,512]{3,2,1,0:T(2,128)(2,1)S(1)} %reshape.64, f32[32,32,2]{1,2,0:T(2,128)S(1)} %copy.101, bf16[32,32,2,256]{3,2,1,0:T(2,128)(2,1)S(1)} %reshape_reshape.7), kind=kOutput, calls=%fused_computation | convolution fusion | flops 3239051264 | bytes 70263040 | tf_op jit(solution)/shard_map/bngk,bngv->bkgv/dot_general | solution.py:81
  217.5 33.7 %copy.103 = f32[32,256,1024]{2,1,0:T(8,128)} copy(f32[32,256,1024]{1,2,0:T(8,128)} %bitcast.39) | data formatting | bytes 67108864
  251.3 51.4 %reduce-scatter.2.cloned.1.call-done = f32[1024,512]{1,0:T(8,128)} async-done(((f32[1024,4096]{1,0:T(8,128)}), f32[1024,512]{1,0:T(8,128)}) %reduce-scatter.2.cloned.1.call-update) | async-done | bytes 2097168 | tf_op jit(solution)/shard_map/reduce_scatter | solution.py:101
  302.7 2.7 convert_element_type.28
  (5 shorter events, 0.0 us)
Async XLA Ops:
  7.2 61.3 %all-gather.2.cloned.1.call-start = ((), (), s32[]{:S(2)}) async-start(), calls=%async_computation.1 | async-start | bytes 9437184 | tf_op jit(solution)/shard_map/all_gather | solution.py:34
  7.9 294.8 %reduce-scatter.2.cloned.1.call-start = ((), (), s32[]{:S(2)}) async-start(), calls=%async_computation.2 | async-start | bytes 18874368 | tf_op jit(solution)/shard_map/reduce_scatter | solution.py:101
  45.6 0.6 copy-start.2
  141.6 3.0 copy-start
  147.9 3.0 copy-start.1
  152.3 3.0 copy-start.4
  186.5 0.7 copy-start.3
Sparse Core Ops, SparseCore 0:
  9.8 58.5 all-gather.1
  186.6 115.9 reduce-scatter.1
where the time goes:
time: 314 us; the launch traced here: 312 us
  matrix products  121 us (39%)
  local copies, waits for them, and re-layouts  98 us (31%)
  waiting for transfers between devices  73 us (23%)
  between operations  14.2 us (5%)
  other arithmetic  5.65 us (2%)
    unnamed x15, local copies, waits for them, and re-layouts  77.5 us
    reduce_scatter x1, waiting for transfers between devices, per_device(): lax.psum_scatter(partial_terms, 'mp', scatter_dimension=1, tiled=True)  51.4 us
    dot_general x3, matrix products, per_device(): updated.append(jnp.dot(segment, weight, preferred_element_type=jnp.float32))  34.7 us
    dot_general x1, matrix products, per_device(): jnp.dot(gated_out, w_out, preferred_element_type=jnp.float32)  31.2 us
    dot_general x1, matrix products, per_device(): jnp.einsum('bngk,bngv->bkgv', decayed_keys, value_block.astype(jnp.float3...  28.9 us
    dot_general x1, matrix products, per_device(): jnp.einsum('bngk,bkgv->bngv', query_block.astype(jnp.float32), old_state,...  21.4 us
    all_gather x1, waiting for transfers between devices, per_device(): segment = lax.all_gather(tokens, 'mp', axis=1, tiled=True)  20.9 us
  transfers between devices with their start and end apart: 2, of which 2 were waited for; matrix products, arithmetic and copies ran while one was open for 33% of the time, Pallas kernels for 0%

commit v1 on v0

--- a/solution.py
+++ b/solution.py
@@ -1,6 +1,10 @@
+import functools
+
 import jax
 import jax.numpy as jnp
 from jax import lax
+from jax.experimental import pallas as pl
+from jax.experimental.pallas import tpu as pltpu
 from jax.sharding import PartitionSpec as P
 
 HEAD = 256
@@ -15,7 +19,7 @@
     return lax.ppermute(shard, axis, [(i, i ^ 1 << bit) for i in range(lax.axis_size(axis))])
 
 
-def per_device(tokens, decay, state, w_query, w_key, w_value, w_gate, w_out, norm_gain):
+def split_heads(tokens, decay, state, w_query, w_key, w_value, w_gate, w_out, norm_gain):
     highest = lax.Precision.HIGHEST
     tok_rows = tokens.shape[0]
     qk_columns = w_query.shape[1]
@@ -104,6 +108,466 @@
     return (layer_out, new_state)
 
 
+CHUNKS = 4
+PER_STEP = 2
+TILE = 512
+
+
+def retention_step(
+    per_step, groups, c_col, c_row, q, k, v, gate, gain, state, *rest
+):
+    gated, new_state = rest[-2:]
+    vw = v.shape[1] // groups
+    rows = lax.broadcasted_iota(jnp.int32, (NEW, NEW), 0)
+    cols = lax.broadcasted_iota(jnp.int32, (NEW, NEW), 1)
+    causal = rows >= cols
+    for s in range(per_step):
+        at = slice(s * NEW, (s + 1) * NEW)
+        for g in range(groups):
+            vs = slice(g * vw, (g + 1) * vw)
+            ks = slice(g * HEAD, (g + 1) * HEAD)
+            col = c_col[at, g : g + 1]
+            row = c_row[s, g : g + 1, :]
+            last = col[NEW - 1 : NEW, :]
+            factor = jnp.where(causal, jnp.exp(jnp.where(causal, col - row, 0.0)), 0.0)
+            query, key, value = q[at, ks], k[at, ks], v[at, vs]
+            scores = lax.dot_general(
+                query, key, (((1,), (1,)), ((), ())), preferred_element_type=jnp.float32
+            )
+            weights = (scores * factor).astype(jnp.bfloat16)
+            old = state[s, :, vs]
+            from_state = jnp.dot(
+                query, old.astype(jnp.bfloat16), preferred_element_type=jnp.float32
+            )
+            in_block = jnp.dot(weights, value, preferred_element_type=jnp.float32)
+            retained = jnp.exp(col) * from_state + in_block
+            scaled = (key.astype(jnp.float32) * jnp.exp(last - col)).astype(jnp.bfloat16)
+            fresh = lax.dot_general(
+                scaled, value, (((0,), (0,)), ((), ())), preferred_element_type=jnp.float32
+            )
+            new_state[s, :, vs] = jnp.exp(last) * old + fresh
+            centre = jnp.mean(retained, axis=1, keepdims=True)
+            deviation = retained - centre
+            variance = jnp.mean(deviation * deviation, axis=1, keepdims=True)
+            normed = deviation * lax.rsqrt(variance + EPS)
+            gates = gate[at, vs]
+            silu = gates / (1.0 + jnp.exp(-gates))
+            gated[at, vs] = (normed * gain[:, vs] * silu).astype(jnp.bfloat16)
+
+
+def retention(chunk, chunks, c_col, c_row, q, k, v, gate, gain, state, previous):
+    rows, groups = c_col.shape
+    sequences = rows // NEW
+    per_step = PER_STEP if sequences % PER_STEP == 0 else 1
+    steps = sequences // per_step
+    step_rows = per_step * NEW
+    qk, vc = q.shape[1], v.shape[1]
+    first = chunk * steps
+    by_row = lambda width: pl.BlockSpec((step_rows, width), lambda i: (i, 0))
+    state_spec = pl.BlockSpec((per_step, HEAD, vc), lambda i: (first + i, 0, 0))
+    in_specs = [
+        by_row(groups),
+        pl.BlockSpec((per_step, groups, NEW), lambda i: (i, 0, 0)),
+        by_row(qk),
+        by_row(qk),
+        by_row(vc),
+        by_row(vc),
+        pl.BlockSpec((1, vc), lambda i: (0, 0)),
+        state_spec,
+    ]
+    operands = [c_col, c_row, q, k, v, gate, gain, state]
+    aliases = {}
+    if previous is not None:
+        in_specs.append(pl.BlockSpec(memory_space=pl.ANY))
+        aliases = {len(operands): 1}
+        operands.append(previous)
+    return pl.pallas_call(
+        functools.partial(retention_step, per_step, groups),
+        grid=(steps,),
+        in_specs=in_specs,
+        out_specs=[by_row(vc), state_spec],
+        out_shape=[
+            jax.ShapeDtypeStruct((rows, vc), jnp.bfloat16),
+            jax.ShapeDtypeStruct(state.shape, jnp.float32),
+        ],
+        input_output_aliases=aliases,
+        compiler_params=pltpu.CompilerParams(
+            dimension_semantics=("arbitrary",), vmem_limit_bytes=40 << 20
+        ),
+        cost_estimate=pl.CostEstimate(
+            flops=12 * rows * HEAD * vc,
+            bytes_accessed=8 * sequences * HEAD * vc,
+            transcendentals=rows * vc,
+        ),
+    )(*operands)
+
+
+def partners(device):
+    core = device % 2
+    across_x = device + 2 - 4 * ((device // 2) % 2)
+    across_y = device + 4 - 8 * (device // 4)
+    near = across_x + core * (across_y - across_x)
+    far = across_y + core * (across_x - across_y)
+    return near, far, across_x + across_y - device, device + 1 - 2 * core
+
+
+def meet(devices):
+    barrier = pltpu.get_barrier_semaphore()
+    for device in devices:
+        pl.semaphore_signal(
+            barrier, inc=1, device_id={"mp": device}, device_id_type=pl.DeviceIdType.MESH
+        )
+    pl.semaphore_wait(barrier, len(devices))
+
+
+def remote(source, target, send, recv, device):
+    return pltpu.make_async_remote_copy(
+        src_ref=source,
+        dst_ref=target,
+        send_sem=send,
+        recv_sem=recv,
+        device_id={"mp": device},
+        device_id_type=pl.DeviceIdType.MESH,
+    )
+
+
+def project_kernel(
+    chunks,
+    tokens,
+    w_query,
+    w_key,
+    w_value,
+    w_gate,
+    query,
+    key_proj,
+    value_proj,
+    gate_proj,
+    gathered,
+    wq,
+    wk,
+    wv,
+    wg,
+    q_held,
+    k_held,
+    v_held,
+    g_held,
+    load_sem,
+    out_sem,
+    send,
+    recv,
+):
+    me = lax.axis_index("mp")
+    near, far, diagonal, sibling = partners(me)
+    sib_near, sib_far, sib_diagonal, _ = partners(sibling)
+    rows, width = tokens.shape
+    size = rows // chunks
+
+    def block(device, r):
+        return gathered.at[
+            pl.ds(pl.multiple_of(r * size, size), size),
+            pl.ds(pl.multiple_of(device * width, width), width),
+        ]
+
+    def copy(lane, source, target, r):
+        there = block(source, r)
+        return remote(there, there, send.at[lane, r], recv.at[lane, r], target)
+
+    own = pltpu.make_async_copy(
+        tokens, gathered.at[:, pl.ds(pl.multiple_of(me * width, width), width)], load_sem.at[0]
+    )
+    own.start()
+    loads = [
+        pltpu.make_async_copy(source, held, load_sem.at[1 + n])
+        for n, (source, held) in enumerate(
+            ((w_query, wq), (w_key, wk), (w_value, wv), (w_gate, wg))
+        )
+    ]
+    for load in loads:
+        load.start()
+    meet((near, far, sibling))
+    own.wait()
+    for r in range(chunks):
+        copy(0, me, near, r).start()
+        if r == 0:
+            copy(1, me, far, r).start()
+        copy(3, me, sibling, r).start()
+
+    def forward(r):
+        copy(0, near, near, r).wait_recv()
+        copy(2, near, far, r).start()
+        copy(4, near, sibling, r).start()
+
+        @pl.when(r + 1 < chunks)
+        def _():
+            copy(1, me, far, r + 1).start()
+
+    def project(r, held, weight, scale, out, n):
+        at = pl.ds(pl.multiple_of(r * size, size), size)
+        for col in range(0, weight.shape[1], TILE):
+            cols = slice(col, min(col + TILE, weight.shape[1]))
+            part = jnp.dot(gathered[at, :], weight[:, cols], preferred_element_type=jnp.float32)
+            if scale is not None:
+                part = part * scale
+            held[at, cols] = part.astype(held.dtype)
+        pltpu.make_async_copy(held.at[at, :], out.at[at, :], out_sem.at[n, r]).start()
+
+    sets = (
+        (q_held, wq, HEAD ** (-0.5), query),
+        (k_held, wk, None, key_proj),
+        (v_held, wv, None, value_proj),
+        (g_held, wg, None, gate_proj),
+    )
+    forward(0)
+
+    def step(r, carry):
+        copy(1, far, far, r).wait_recv()
+        copy(5, far, sibling, r).start()
+        copy(2, diagonal, far, r).wait_recv()
+        copy(6, diagonal, sibling, r).start()
+
+        @pl.when(r + 1 < chunks)
+        def _():
+            forward(r + 1)
+
+        copy(3, sibling, sibling, r).wait_recv()
+        copy(4, sib_near, sibling, r).wait_recv()
+        copy(5, sib_far, sibling, r).wait_recv()
+        copy(6, sib_diagonal, sibling, r).wait_recv()
+        for n, (held, weight, scale, out) in enumerate(sets):
+
+            @pl.when(r == 0)
+            def _():
+                loads[n].wait()
+
+            project(r, held, weight, scale, out, n)
+        return carry
+
+    lax.fori_loop(0, chunks, step, 0)
+
+    def drain(r, carry):
+        at = pl.ds(pl.multiple_of(r * size, size), size)
+        for lane, (source, target) in enumerate(
+            (
+                (me, near),
+                (me, far),
+                (near, far),
+                (me, sibling),
+                (near, sibling),
+                (far, sibling),
+                (diagonal, sibling),
+            )
+        ):
+            copy(lane, source, target, r).wait_send()
+        for n, (held, weight, scale, out) in enumerate(sets):
+            pltpu.make_async_copy(held.at[at, :], out.at[at, :], out_sem.at[n, r]).wait()
+        return carry
+
+    lax.fori_loop(0, chunks, drain, 0)
+
+
+def gather_project(tokens, w_query, w_key, w_value, w_gate):
+    rows, width = tokens.shape
+    depth, qk = w_query.shape
+    vc = w_value.shape[1]
+    chunks = CHUNKS
+    shapes = [
+        ((rows, qk), jnp.bfloat16),
+        ((rows, qk), jnp.bfloat16),
+        ((rows, vc), jnp.bfloat16),
+        ((rows, vc), jnp.float32),
+    ]
+    anywhere = pl.BlockSpec(memory_space=pl.ANY)
+    return pl.pallas_call(
+        functools.partial(project_kernel, chunks),
+        in_specs=[anywhere] * 5,
+        out_specs=[anywhere] * 4,
+        out_shape=[jax.ShapeDtypeStruct(*shape) for shape in shapes],
+        scratch_shapes=[
+            pltpu.VMEM((rows, depth), jnp.bfloat16),
+            pltpu.VMEM((depth, qk), jnp.bfloat16),
+            pltpu.VMEM((depth, qk), jnp.bfloat16),
+            pltpu.VMEM((depth, vc), jnp.bfloat16),
+            pltpu.VMEM((depth, vc), jnp.bfloat16),
+        ]
+        + [pltpu.VMEM(*shape) for shape in shapes]
+        + [
+            pltpu.SemaphoreType.DMA((5,)),
+            pltpu.SemaphoreType.DMA((4, chunks)),
+            pltpu.SemaphoreType.DMA((7, chunks)),
+            pltpu.SemaphoreType.DMA((7, chunks)),
+        ],
+        compiler_params=pltpu.CompilerParams(
+            collective_id=0, has_side_effects=True, vmem_limit_bytes=56 << 20
+        ),
+    )(tokens, w_query, w_key, w_value, w_gate)
+
+
+def output_kernel(
+    chunks,
+    gated,
+    w_out,
+    layer_out,
+    gated_held,
+    w_held,
+    to_sibling,
+    from_sibling,
+    outgoing,
+    incoming,
+    total,
+    load_sem,
+    send,
+    recv,
+):
+    me = lax.axis_index("mp")
+    near, far, diagonal, sibling = partners(me)
+    sib_near, sib_far, sib_diagonal, _ = partners(sibling)
+    width = layer_out.shape[1]
+    rows = gated.shape[0]
+    size = rows // chunks
+    loads = [
+        pltpu.make_async_copy(gated, gated_held, load_sem.at[0]),
+        pltpu.make_async_copy(w_out, w_held, load_sem.at[1]),
+    ]
+    for load in loads:
+        load.start()
+    meet((near, far, sibling))
+    for load in loads:
+        load.wait()
+    mine = (me, near, far, diagonal)
+    theirs = (sibling, sib_near, sib_far, sib_diagonal)
+
+    def at(r):
+        return pl.ds(pl.multiple_of(r * size, size), size)
+
+    def share(dest, r):
+        return jnp.dot(
+            gated_held[at(r), :],
+            w_held[:, pl.ds(pl.multiple_of(dest * width, width), width)],
+            preferred_element_type=jnp.float32,
+        )
+
+    def swap(j, r):
+        return remote(
+            to_sibling.at[j, at(r), :],
+            from_sibling.at[j, at(r), :],
+            send.at[j, r],
+            recv.at[j, r],
+            sibling,
+        )
+
+    def hop(lane, r):
+        return remote(
+            outgoing.at[lane, at(r), :],
+            incoming.at[lane, at(r), :],
+            send.at[4 + lane, r],
+            recv.at[4 + lane, r],
+            near if lane == 0 else far,
+        )
+
+    for j in (3, 2, 1, 0):
+
+        def give(r, carry):
+            to_sibling[j, at(r), :] = share(theirs[j], r).astype(jnp.bfloat16)
+            swap(j, r).start()
+            return carry
+
+        def combine(r, carry):
+            part = share(mine[j], r)
+            swap(j, r).wait_recv()
+            part = part + from_sibling[j, at(r), :].astype(jnp.float32)
+            if j == 1:
+                hop(2, r).wait_recv()
+                part = part + incoming[2, at(r), :].astype(jnp.float32)
+            if j == 0:
+                total[at(r), :] = part
+            else:
+                outgoing[j - 1, at(r), :] = part.astype(jnp.bfloat16)
+                hop(j - 1, r).start()
+            return carry
+
+        lax.fori_loop(0, chunks, give, 0)
+        lax.fori_loop(0, chunks, combine, 0)
+
+    def finish(r, carry):
+        hop(1, r).wait_recv()
+        hop(0, r).wait_recv()
+        layer_out[at(r), :] = (
+            total[at(r), :]
+            + incoming[0, at(r), :].astype(jnp.float32)
+            + incoming[1, at(r), :].astype(jnp.float32)
+        ).astype(jnp.bfloat16)
+        for j in range(4):
+            swap(j, r).wait_send()
+        for lane in range(3):
+            hop(lane, r).wait_send()
+        return carry
+
+    lax.fori_loop(0, chunks, finish, 0)
+
+
+def project_out(gated, w_out, width):
+    rows = gated.shape[0]
+    chunks = CHUNKS
+    anywhere = pl.BlockSpec(memory_space=pl.ANY)
+    return pl.pallas_call(
+        functools.partial(output_kernel, chunks),
+        in_specs=[anywhere] * 2,
+        out_specs=pl.BlockSpec(memory_space=pltpu.VMEM),
+        out_shape=jax.ShapeDtypeStruct((rows, width), jnp.bfloat16),
+        scratch_shapes=[
+            pltpu.VMEM(gated.shape, jnp.bfloat16),
+            pltpu.VMEM(w_out.shape, jnp.bfloat16),
+            pltpu.VMEM((4, rows, width), jnp.bfloat16),
+            pltpu.VMEM((4, rows, width), jnp.bfloat16),
+            pltpu.VMEM((3, rows, width), jnp.bfloat16),
+            pltpu.VMEM((3, rows, width), jnp.bfloat16),
+            pltpu.VMEM((rows, width), jnp.float32),
+            pltpu.SemaphoreType.DMA((2,)),
+            pltpu.SemaphoreType.DMA((7, chunks)),
+            pltpu.SemaphoreType.DMA((7, chunks)),
+        ],
+        compiler_params=pltpu.CompilerParams(
+            collective_id=1, has_side_effects=True, vmem_limit_bytes=56 << 20
+        ),
+    )(gated, w_out)
+
+
+def whole_heads(tokens, decay, state, w_query, w_key, w_value, w_gate, w_out, norm_gain):
+    tok_rows = tokens.shape[0]
+    groups = w_query.shape[1] // HEAD
+    sequences = tok_rows // NEW
+    first_head = lax.axis_index("mp") * groups
+    logs = jnp.log(lax.dynamic_slice_in_dim(decay, first_head, groups, 1))
+    logs = logs.reshape(sequences, NEW, groups)
+    causal = jnp.arange(NEW)[:, None] >= jnp.arange(NEW)[None, :]
+    cumul = jnp.sum(jnp.where(causal[None, :, :, None], logs[:, None], 0.0), axis=2)
+    c_col = cumul.reshape(tok_rows, groups)
+    c_row = jnp.transpose(cumul, (0, 2, 1))
+    query, key_proj, value_proj, gate_proj = gather_project(
+        tokens, w_query, w_key, w_value, w_gate
+    )
+    gated_out, new_state = retention(
+        0,
+        1,
+        c_col,
+        c_row,
+        query,
+        key_proj,
+        value_proj,
+        gate_proj,
+        norm_gain.reshape(1, -1),
+        state,
+        None,
+    )
+    return (project_out(gated_out, w_out, tokens.shape[1]), new_state)
+
+
+def per_device(tokens, decay, state, w_query, *rest):
+    whole = w_query.shape[1] % HEAD == 0 and lax.axis_size("mp") == 8
+    path = whole_heads if whole else split_heads
+    return path(tokens, decay, state, w_query, *rest)
+
+
 def solution(mesh):
     placed = (
         P("dp", "mp"),

time: 314 us -> 145 us (0.46)
  Pallas kernels: 0 us -> 132 us
  matrix products: 121 us -> 0 us
  local copies, waits for them, and re-layouts: 98 us -> 11 us
  waiting for transfers between devices: 73 us -> 0 us
  between operations: 14.2 us -> 0.7 us
  other arithmetic: 5.65 us -> 0.4 us
    pallas_call x0 -> x3, Pallas kernels: none -> 132 us  [the longest x1 55.7 us: gather_project(): pl.pallas_call(functools.partial(project_kernel, chunks), in_specs=[anywh...]
    dot_general x7 -> x0, matrix products: 121 us -> none  [the longest x3 34.7 us: per_device(): updated.append(jnp.dot(segment, weight, preferred_element_type=jnp.float32))]
    unnamed x15 -> x13, local copies, waits for them, and re-layouts: 77.5 us -> 9.83 us
    reduce_scatter x1 -> x0, waiting for transfers between devices: 51.4 us -> none  [per_device(): lax.psum_scatter(partial_terms, 'mp', scatter_dimension=1, tiled=True)]
    all_gather x1 -> x0, waiting for transfers between devices: 20.9 us -> none  [per_device(): segment = lax.all_gather(tokens, 'mp', axis=1, tiled=True)]
    another operation x2 -> x0, local copies, waits for them, and re-layouts: 3.56 us -> none  [the longest x1 2.22 us: per_device(): query_block = query.reshape(sequences, NEW, groups, HEAD)]
    add x1 -> x0, local copies, waits for them, and re-layouts: 3.34 us -> none  [per_device(): retained = jnp.exp(log_cumul)[..., None] * from_state + in_block]
  transfers between devices with their start and end apart: 2 -> 0, of which waited for: 2 -> 0; matrix products, arithmetic and copies ran while one was open for 33% -> 0% of each run, Pallas kernels for 0% -> 0%
where the time goes in v1:
time: 145 us; the launch traced here: 144 us
  Pallas kernels  132 us (91%)
  local copies, waits for them, and re-layouts  11 us (8%)
    pallas_call x1, Pallas kernels, gather_project(): pl.pallas_call(functools.partial(project_kernel, chunks), in_specs=[anywh...  55.7 us
    pallas_call x1, Pallas kernels, project_out(): pl.pallas_call(functools.partial(output_kernel, chunks), in_specs=[anywhe...  43.9 us
    pallas_call x1, Pallas kernels, retention(): pl.pallas_call(functools.partial(retention_step, per_step, groups), grid=...  32.1 us
    unnamed x13, local copies, waits for them, and re-layouts  9.83 us

profile of v1, /device:TPU:0, one launch (start us, length us, event | category | flops | bytes accessed | tf_op | source)
XLA Modules:
  0.0 143.8 jit_solution(11396791030830854516)
XLA Ops:
  0.6 0.8 dynamic-slice_log_fusion
  1.4 0.1 broadcast_in_dim.26
  1.5 0.4 select_reduce_fusion
  1.9 0.3 copy.18
  2.2 0.0 copy-start.5
  2.2 55.7 %shard_map.104 = (bf16[1024,512]{1,0:T(8,128)(2,1)}, bf16[1024,512]{1,0:T(8,128)(2,1)}, bf16[1024,1024]{1,0:T(8,128)(2,1)}, f32[1024,1024]{1,0:T(8,128)}) custom-call(bf16[1024,512]{1,0:T(8,128)(2,1)} %tokens.1, bf16[4096,512]{1,0:T(8,128)(2,1)} %w_query.1, bf16[4096,512]{1,0:T(8,128)(2,1)} %w_key.1, bf16[4096,1024]{1,0:T(8,128)(2,1)} %w_value.1, ...), custom_call_target="tpu_custom_call" | custom-call | tf_op jit(solution)/shard_map/pallas_call | solution.py:380
  57.9 0.0 copy-done.5
  57.9 0.0 copy-start
  58.0 2.2 %copy-done = f32[1024,1024]{1,0:T(8,128)S(1)} copy-done((f32[1024,1024]{1,0:T(8,128)S(1)}, f32[1024,1024]{1,0:T(8,128)}, u32[]{:S(2)}) %copy-start) | copy-done | bytes 4194328
  60.1 0.0 copy-start.1
  60.1 1.6 %copy-done.1 = bf16[1024,1024]{1,0:T(8,128)(2,1)S(1)} copy-done((bf16[1024,1024]{1,0:T(8,128)(2,1)S(1)}, bf16[1024,1024]{1,0:T(8,128)(2,1)}, u32[]{:S(2)}) %copy-start.1) | copy-done | bytes 2097176
  61.7 0.0 copy-start.3
  61.7 1.2 copy-done.3
  63.0 0.0 copy-start.4
  63.0 1.2 copy-done.4
  64.2 32.1 %shard_map.105 = (bf16[1024,1024]{1,0:T(8,128)(2,1)S(1)}, f32[32,256,1024]{2,1,0:T(8,128)}) custom-call(f32[1024,2]{1,0:T(8,128)S(1)} %bitcast.5, f32[32,2,32]{2,1,0:T(2,128)S(1)} %bitcast.6, bf16[1024,512]{1,0:T(8,128)(2,1)S(1)} %copy-done.3, bf16[1024,512]{1,0:T(8,128)(2,1)S(1)} %copy-done.4, bf16[1024,1024]{1,0:T(8,128)(2,1)S(1)} %copy-done.1, ...), custom_call_target="tpu_custom_call" | custom-call | flops 3221225472 | bytes 67108864 | tf_op jit(solution)/shard_map/pallas_call | solution.py:184
  96.2 0.0 copy-start.2
  96.2 1.3 copy-done.2
  97.6 43.9 %shard_map.106 = bf16[1024,512]{1,0:T(8,128)(2,1)} custom-call(bf16[1024,1024]{1,0:T(8,128)(2,1)} %copy-done.2, bf16[1024,4096]{1,0:T(8,128)(2,1)} %w_out.1), custom_call_target="tpu_custom_call" | custom-call | tf_op jit(solution)/shard_map/pallas_call | solution.py:512
  141.5 2.3 %copy.21 = bf16[1024,512]{1,0:T(8,128)(2,1)} copy(bf16[1024,512]{1,0:T(8,128)(2,1)} %shard_map.106) | data formatting | bytes 2097152
  (2 shorter events, 0.0 us)
Async XLA Ops:
  2.2 55.7 %copy-start.5 = (f32[1024]{0:T(1024)S(1)}, f32[1024]{0:T(1024)}, u32[]{:S(2)}) copy-start(f32[1024]{0:T(1024)} %param.17) | copy-start | bytes 12292
  57.9 2.2 %copy-start = (f32[1024,1024]{1,0:T(8,128)S(1)}, f32[1024,1024]{1,0:T(8,128)}, u32[]{:S(2)}) copy-start(f32[1024,1024]{1,0:T(8,128)} %get-tuple-element.11.gate) | copy-start | bytes 12582916
  60.1 1.6 %copy-start.1 = (bf16[1024,1024]{1,0:T(8,128)(2,1)S(1)}, bf16[1024,1024]{1,0:T(8,128)(2,1)}, u32[]{:S(2)}) copy-start(bf16[1024,1024]{1,0:T(8,128)(2,1)} %get-tuple-element.10.v) | copy-start | bytes 6291460
  61.7 1.2 copy-start.3
  63.0 1.2 copy-start.4
  96.2 1.3 copy-start.2
